TPU v7x, 64 devices: a 2x2x8 block of a 4x4x8 slice. The times are simulated.
64 devices in a mesh: dp: 4 (over x, y), w: 16 (over z, core).
Axes of the slice: x: 2, y: 2, z: 8, core: 2. Of those that a mesh axis runs over, the one named last changes fastest.
The devices are a block of a 4x4x8 slice.
Arguments:
- hidden: bfloat16 [1024, 64, 1152], P(('dp', 'w')), parts along dimension 0
- lengths: int32 [1024], P(('dp', 'w')), parts along dimension 0
- attn_norm: bfloat16 [2, 1152], P(None, 'w')
- w_q: bfloat16 [2, 1152, 1024], P(None, 'w')
- w_k: bfloat16 [2, 1152, 256], P(None, 'w')
- w_v: bfloat16 [2, 1152, 256], P(None, 'w')
- w_o: bfloat16 [2, 1024, 1152], P(None, 'w')
- mlp_norm: bfloat16 [2, 1152], P(None, 'w')
- w_gate: bfloat16 [2, 1152, 6912], P(None, 'w')
- w_up: bfloat16 [2, 1152, 6912], P(None, 'w')
- w_down: bfloat16 [2, 6912, 1152], P(None, 'w')
Outputs:
- output 1: bfloat16 [1024, 64, 1152], P(('dp', 'w')), parts along dimension 0
- output 2: bfloat16 [2, 1024, 64, 1, 256], P(None, ('dp', 'w')), parts along dimension 1
- output 3: bfloat16 [2, 1024, 64, 1, 256], P(None, ('dp', 'w')), parts along dimension 1
There are 4 independent parts. A program takes and returns all parts, laid end to end along the dimension named above; an argument that names none is the same for every part.
All inputs are finite; a program needn't handle non-finite values.
Results may differ from a plain program's by a relative error of at most 0.0130315.
Values are sent between devices in bfloat16 or wider.
A program may use at most 768 MiB of HBM per device.

v0:
```python
import jax
import jax.numpy as jnp
from jax import lax
from jax.sharding import PartitionSpec as P

HEAD_DIM = 256
RMS_EPS = 1e-6
ROPE_THETA = 10000.0
QUERY_BLOCK = 512


def rms_norm(hidden_f, norm_gain):
    mean_sq = jnp.mean(hidden_f * hidden_f, axis=-1, keepdims=True)
    return (hidden_f * lax.rsqrt(mean_sq + RMS_EPS) * (1.0 + norm_gain.astype(jnp.float32))).astype(jnp.bfloat16)


def rope_tables(seq_len):
    half_dim = HEAD_DIM // 2
    inv_freq = ROPE_THETA ** (-2.0 * jnp.arange(half_dim, dtype=jnp.float32) / HEAD_DIM)
    angles = jnp.arange(seq_len, dtype=jnp.float32)[:, None] * inv_freq[None, :]
    return jnp.cos(angles)[:, None, :], jnp.sin(angles)[:, None, :]


def apply_rope(projected, cos_tab, sin_tab):
    half_dim = HEAD_DIM // 2
    first_half = projected[..., :half_dim]
    second_half = projected[..., half_dim:]
    return jnp.concatenate([first_half * cos_tab - second_half * sin_tab, second_half * cos_tab + first_half * sin_tab], axis=-1)


def attention(q_rope, k_rope, v_proj, lengths):
    seq_len = q_rope.shape[1]
    q_block = min(seq_len, QUERY_BLOCK)
    pieces = []
    for q_start in range(0, seq_len, q_block):
        q_stop = q_start + q_block
        scores = jnp.einsum('bqhgd,bshd->bhgqs', q_rope[:, q_start:q_stop], k_rope[:, :q_stop], preferred_element_type=jnp.float32)
        q_pos = q_start + jnp.arange(q_block)
        k_pos = jnp.arange(q_stop)
        allowed = (k_pos[None, None, :] <= q_pos[None, :, None]) & (k_pos[None, None, :] < lengths[:, None, None])
        scores = jnp.where(allowed[:, None, None], scores, -1e30)
        scores = scores - jnp.max(scores, axis=-1, keepdims=True)
        exp_scores = jnp.exp(scores)
        attn_probs = exp_scores / jnp.sum(exp_scores, axis=-1, keepdims=True)
        row_live = q_pos[None, :] < lengths[:, None]
        attn_probs = jnp.where(row_live[:, None, None, :, None], attn_probs, 0.0).astype(jnp.bfloat16)
        pieces.append(jnp.einsum('bhgqs,bshd->bqhgd', attn_probs, v_proj[:, :q_stop], preferred_element_type=jnp.float32).astype(jnp.bfloat16))
    return jnp.concatenate(pieces, axis=1)


def mlp_block(mixed_bf, mlp_gain, wg_full, wu_full, wd_full):
    mixed_f = mixed_bf.astype(jnp.float32)
    normed = rms_norm(mixed_f, mlp_gain)
    gate_proj = jnp.einsum('bsd,df->bsf', normed, wg_full, preferred_element_type=jnp.float32)
    up_proj = jnp.einsum('bsd,df->bsf', normed, wu_full, preferred_element_type=jnp.float32)
    act_bf = (jax.nn.gelu(gate_proj, approximate=True) * up_proj).astype(jnp.bfloat16)
    return (mixed_f + jnp.einsum('bsf,fd->bsd', act_bf, wd_full, preferred_element_type=jnp.float32)).astype(jnp.bfloat16)


def layer_body(hidden, lengths, weights):
    attn_gain, wq_full, wk_full, wv_full, wo_full, mlp_gain, wg_full, wu_full, wd_full = weights
    n_seq = hidden.shape[0]
    seq_len = hidden.shape[1]
    n_heads = wq_full.shape[1] // HEAD_DIM
    kv_heads = wk_full.shape[1] // HEAD_DIM
    cos_tab, sin_tab = rope_tables(seq_len)
    hidden_f = hidden.astype(jnp.float32)
    normed = rms_norm(hidden_f, attn_gain)
    q_proj = jnp.einsum('bsd,de->bse', normed, wq_full, preferred_element_type=jnp.float32).reshape(n_seq, seq_len, n_heads, HEAD_DIM)
    k_proj = jnp.einsum('bsd,de->bse', normed, wk_full, preferred_element_type=jnp.float32).reshape(n_seq, seq_len, kv_heads, HEAD_DIM)
    v_proj = jnp.einsum('bsd,de->bse', normed, wv_full, preferred_element_type=jnp.float32).astype(jnp.bfloat16).reshape(n_seq, seq_len, kv_heads, HEAD_DIM)
    q_rope = (apply_rope(q_proj, cos_tab, sin_tab) * HEAD_DIM ** -0.5).astype(jnp.bfloat16).reshape(n_seq, seq_len, kv_heads, n_heads // kv_heads, HEAD_DIM)
    k_rope = apply_rope(k_proj, cos_tab, sin_tab).astype(jnp.bfloat16)
    attn_out = attention(q_rope, k_rope, v_proj, lengths).reshape(n_seq, seq_len, n_heads * HEAD_DIM)
    mixed_bf = (hidden_f + jnp.einsum('bse,ed->bsd', attn_out, wo_full, preferred_element_type=jnp.float32)).astype(jnp.bfloat16)
    return mlp_block(mixed_bf, mlp_gain, wg_full, wu_full, wd_full), k_rope, v_proj


def solution(mesh):
    batch_spec = P(('dp', 'w'))
    weight_spec = P(None, 'w')
    cache_spec = P(None, ('dp', 'w'))

    def device_fn(hidden, lengths, attn_norm, w_q, w_k, w_v, w_o, mlp_norm, w_gate, w_up, w_down):
        k_list = []
        v_list = []
        for layer_idx in range(w_q.shape[0]):
            gathered = [lax.all_gather(weight[layer_idx], 'w', axis=0, tiled=True) for weight in (attn_norm, w_q, w_k, w_v, w_o, mlp_norm, w_gate, w_up, w_down)]
            hidden, k_rope, v_proj = layer_body(hidden, lengths, gathered)
            k_list.append(k_rope)
            v_list.append(v_proj)
        return hidden, jnp.stack(k_list), jnp.stack(v_list)

    return jax.shard_map(device_fn, mesh=mesh, in_specs=(batch_spec, batch_spec) + (weight_spec,) * 9, out_specs=(batch_spec, cache_spec, cache_spec), check_vma=False)
```

profile of v0, /device:TPU:30, one launch (start us, length us, event | category | flops | bytes accessed | tf_op | source)
XLA Modules:
  0.0 731.5 jit_solution(7190800145256887774)
XLA Ops:
  24.7 53.0 %all-reduce.4 = (bf16[1152]{0:T(1024)(128)(2,1)S(1)}, bf16[1152]{0:T(1024)(128)(2,1)S(1)}, bf16[1152]{0:T(1024)(128)(2,1)S(1)}, bf16[1152]{0:T(1024)(128)(2,1)S(1)}) all-reduce(bf16[1152]{0:T(1024)(128)(2,1)S(1)} %dynamic-update-slice, bf16[1152]{0:T(1024)(128)(2,1)S(1)} %dynamic-update-slice.1, ...), channel_id=2, replica_groups=mesh['dp'=4,'w'=16] {'w'}, use_global_device_ids=true, to_apply=%add | all-reduce | flops 4608 | bytes 18432
  78.4 16.0 %all-gather.2 = bf16[1,1152,256]{2,1,0:T(8,128)(2,1)S(1)} all-gather(bf16[1,72,256]{2,1,0:T(8,128)(2,1)S(1)} %get-tuple-element.38), channel_id=4, replica_groups=mesh['dp'=4,'w'=16] {'w'}, dimensions={1}, use_global_device_ids=true | all-gather | bytes 626688 | tf_op jit(solution)/shard_map/all_gather | solution.py:88
  94.6 21.0 %all-gather.1 = bf16[1,1152,256]{2,1,0:T(8,128)(2,1)S(1)} all-gather(bf16[1,72,256]{2,1,0:T(8,128)(2,1)S(1)} %get-tuple-element.36), channel_id=3, replica_groups=mesh['dp'=4,'w'=16] {'w'}, dimensions={1}, use_global_device_ids=true | all-gather | bytes 626688 | tf_op jit(solution)/shard_map/all_gather | solution.py:88
  118.8 19.6 %all-gather.11 = bf16[1,1152,256]{2,1,0:T(8,128)(2,1)} all-gather(bf16[1,72,256]{2,1,0:T(8,128)(2,1)S(1)} %get-tuple-element.37), channel_id=13, replica_groups=mesh['dp'=4,'w'=16] {'w'}, dimensions={1}, use_global_device_ids=true | all-gather | bytes 626688 | tf_op jit(solution)/shard_map/all_gather | solution.py:88
  138.3 21.3 %all-gather.10 = bf16[1,1152,256]{2,1,0:T(8,128)(2,1)} all-gather(bf16[1,72,256]{2,1,0:T(8,128)(2,1)S(1)} %get-tuple-element.35), channel_id=12, replica_groups=mesh['dp'=4,'w'=16] {'w'}, dimensions={1}, use_global_device_ids=true | all-gather | bytes 626688 | tf_op jit(solution)/shard_map/all_gather | solution.py:88
  160.6 6.3 fusion.68
  167.0 5.7 reshape.301
  183.4 6.0 fusion.42
  189.5 26.3 %fusion.26 = f32[16,64,6912]{2,1,0:T(8,128)} fusion(bf16[1,1152,6912]{2,1,0:T(8,128)(2,1)} %all-gather.35.cloned.1.call-done, bf16[16,64,1152]{2,1,0:T(8,128)(2,1)S(1)} %get-tuple-element.48, f32[1152]{0:T(1024)S(1)} %convert_add_fusion.6, f32[16,64]{1,0:T(8,128)S(1)} %add_rsqrt_fusion.2), kind=kOutput, calls=%fused_computation.27 | convolution fusion | flops 16312172544 | bytes 46604800 | tf_op jit(solution)/shard_map/bsd,df->bsf/dot_general | solution.py:55
  215.8 56.6 %all-gather.33.cloned.1.call-done = bf16[1,1152,6912]{2,1,0:T(8,128)(2,1)} async-done(((bf16[1,72,6912]{2,1,0:T(8,128)(2,1)}), bf16[1,1152,6912]{2,1,0:T(8,128)(2,1)}) %all-gather.33.cloned.1.call-update) | async-done | bytes 15925264 | tf_op jit(solution)/shard_map/all_gather | solution.py:88
  272.4 32.3 %fusion.8.clone.3.clone.4 = bf16[16,64,6912]{2,1,0:T(8,128)(2,1)} fusion(f32[16,64,6912]{2,1,0:T(8,128)} %fusion.26, bf16[1,1152,6912]{2,1,0:T(8,128)(2,1)} %all-gather.33.cloned.1.call-done, bf16[16,64,1152]{2,1,0:T(8,128)(2,1)S(1)} %get-tuple-element.48, f32[1152]{0:T(1024)S(1)} %convert_add_fusion.6, ...), kind=kOutput, calls=%fused_computation.10.clone.clone.clone.clone.clone.clone.clone.1 | convolution fusion | flops 16382951424 | bytes 60760576 | tf_op jit(solution)/shard_map/bsd,df->bsf/dot_general | solution.py:54
  304.7 56.3 %all-gather.37.cloned.1.call-done = bf16[1,6912,1152]{2,1,0:T(8,128)(2,1)} async-done(((bf16[1,432,1152]{2,1,0:T(8,128)(2,1)}), bf16[1,6912,1152]{2,1,0:T(8,128)(2,1)}) %all-gather.37.cloned.1.call-update) | async-done | bytes 15925264 | tf_op jit(solution)/shard_map/all_gather | solution.py:88
  361.0 26.8 %fusion.46 = (f32[16,64]{1,0:T(8,128)S(1)}, bf16[16,64,1152]{2,1,0:T(8,128)(2,1)}) fusion(bf16[1,6912,1152]{2,1,0:T(8,128)(2,1)} %all-gather.37.cloned.1.call-done, bf16[16,64,1152]{2,1,0:T(8,128)(2,1)} %copy-done.23, bf16[16,64,6912]{2,1,0:T(8,128)(2,1)} %fusion.8.clone.3.clone.4), kind=kOutput, calls=%fused_computation.58 | convolution fusion | flops 16314530816 | bytes 34803712 | tf_op jit(solution)/shard_map/bsf,fd->bsd/dot_general | solution.py:57
  387.8 9.9 %all-gather.39.cloned.1.call-done = bf16[1,1152,1024]{2,1,0:T(8,128)(2,1)} async-done(((bf16[1,72,1024]{2,1,0:T(8,128)(2,1)}), bf16[1,1152,1024]{2,1,0:T(8,128)(2,1)}) %all-gather.39.cloned.1.call-update) | async-done | bytes 2359312 | tf_op jit(solution)/shard_map/all_gather | solution.py:88
  397.7 7.3 fusion.65
  404.9 5.7 reshape.305
  427.4 6.6 all-gather.41.cloned.1.call-done
  434.1 6.3 fusion.50
  440.3 81.5 %all-gather.45.cloned.1.call-done = bf16[1,1152,6912]{2,1,0:T(8,128)(2,1)} async-done(((bf16[1,72,6912]{2,1,0:T(8,128)(2,1)}), bf16[1,1152,6912]{2,1,0:T(8,128)(2,1)}) %all-gather.45.cloned.1.call-update) | async-done | bytes 15925264 | tf_op jit(solution)/shard_map/all_gather | solution.py:88
  521.8 26.6 %fusion.21 = f32[16,64,6912]{2,1,0:T(8,128)} fusion(bf16[1,1152,6912]{2,1,0:T(8,128)(2,1)} %all-gather.45.cloned.1.call-done, bf16[16,64,1152]{2,1,0:T(8,128)(2,1)} %get-tuple-element.54, f32[1152]{0:T(1024)S(1)} %copy-done.16, f32[16,64]{1,0:T(8,128)S(1)} %add_rsqrt_fusion), kind=kOutput, calls=%fused_computation.23 | convolution fusion | flops 16312172544 | bytes 46604800 | tf_op jit(solution)/shard_map/bsd,df->bsf/dot_general | solution.py:55
  548.4 61.6 %all-gather.43.cloned.1.call-done = bf16[1,1152,6912]{2,1,0:T(8,128)(2,1)} async-done(((bf16[1,72,6912]{2,1,0:T(8,128)(2,1)}), bf16[1,1152,6912]{2,1,0:T(8,128)(2,1)}) %all-gather.43.cloned.1.call-update) | async-done | bytes 15925264 | tf_op jit(solution)/shard_map/all_gather | solution.py:88
  610.0 31.4 %fusion.17.clone.6 = bf16[16,64,6912]{2,1,0:T(8,128)(2,1)} fusion(f32[16,64,6912]{2,1,0:T(8,128)} %fusion.21, bf16[1,1152,6912]{2,1,0:T(8,128)(2,1)} %all-gather.43.cloned.1.call-done, bf16[16,64,1152]{2,1,0:T(8,128)(2,1)} %get-tuple-element.54, f32[1152]{0:T(1024)S(1)} %copy-done.16, f32[16,64]{1,0:T(8,128)S(1)} %add_rsqrt_fusion), kind=kOutput, calls=%fused_computation.19.clone.clone.clone.clone.clone.1 | convolution fusion | flops 16382951424 | bytes 60760576 | tf_op jit(solution)/shard_map/bsd,df->bsf/dot_general | solution.py:54
  641.5 56.6 %all-gather.47.cloned.1.call-done = bf16[1,6912,1152]{2,1,0:T(8,128)(2,1)} async-done(((bf16[1,432,1152]{2,1,0:T(8,128)(2,1)}), bf16[1,6912,1152]{2,1,0:T(8,128)(2,1)}) %all-gather.47.cloned.1.call-update) | async-done | bytes 15925264 | tf_op jit(solution)/shard_map/all_gather | solution.py:88
  698.1 26.4 %fusion.53 = bf16[16,64,1152]{2,1,0:T(8,128)(2,1)} fusion(bf16[16,64,1152]{2,1,0:T(8,128)(2,1)} %get-tuple-element.54, bf16[1,6912,1152]{2,1,0:T(8,128)(2,1)} %all-gather.47.cloned.1.call-done, bf16[16,64,6912]{2,1,0:T(8,128)(2,1)} %fusion.17.clone.6), kind=kOutput, calls=%fused_computation.65 | convolution fusion | flops 16310992896 | bytes 34799616 | tf_op jit(solution)/shard_map/bsf,fd->bsd/dot_general | solution.py:57
  (125 shorter events, 49.0 us)
Async XLA Ops:
  7.2 153.4 %all-gather.29.cloned.1.call-start = ((), (), s32[]{:S(2)}) async-start(), calls=%async_computation | async-start | bytes 2506752 | tf_op jit(solution)/shard_map/all_gather | solution.py:88
  9.0 174.4 %all-gather.31.cloned.1.call-start = ((), (), s32[]{:S(2)}) async-start(), calls=%async_computation.1 | async-start | bytes 2506752 | tf_op jit(solution)/shard_map/all_gather | solution.py:88
  10.9 178.6 %all-gather.35.cloned.1.call-start = ((), (), s32[]{:S(2)}) async-start(), calls=%async_computation.3 | async-start | bytes 16920576 | tf_op jit(solution)/shard_map/all_gather | solution.py:88
  14.1 258.3 %all-gather.33.cloned.1.call-start = ((), (), s32[]{:S(2)}) async-start(), calls=%async_computation.2 | async-start | bytes 16920576 | tf_op jit(solution)/shard_map/all_gather | solution.py:88
  15.6 345.4 %all-gather.37.cloned.1.call-start = ((), (), s32[]{:S(2)}) async-start(), calls=%async_computation.4 | async-start | bytes 16920576 | tf_op jit(solution)/shard_map/all_gather | solution.py:88
  18.6 59.1 %copy-start.1 = (bf16[16,64,1152]{2,1,0:T(8,128)(2,1)S(1)}, bf16[16,64,1152]{2,1,0:T(8,128)(2,1)}, u32[]{:S(2)}) copy-start(bf16[16,64,1152]{2,1,0:T(8,128)(2,1)} %param.11) | copy-start | bytes 7077892
  18.7 379.0 %all-gather.39.cloned.1.call-start = ((), (), s32[]{:S(2)}) async-start(), calls=%async_computation.5 | async-start | bytes 2506752 | tf_op jit(solution)/shard_map/all_gather | solution.py:88
  19.3 414.7 %all-gather.41.cloned.1.call-start = ((), (), s32[]{:S(2)}) async-start(), calls=%async_computation.6 | async-start | bytes 2506752 | tf_op jit(solution)/shard_map/all_gather | solution.py:88
  20.1 501.7 %all-gather.45.cloned.1.call-start = ((), (), s32[]{:S(2)}) async-start(), calls=%async_computation.8 | async-start | bytes 16920576 | tf_op jit(solution)/shard_map/all_gather | solution.py:88
  20.9 57.4 %copy-start.12 = (bf16[2,72,256]{2,1,0:T(8,128)(2,1)S(1)}, bf16[2,72,256]{2,1,0:T(8,128)(2,1)}, u32[]{:S(2)}) copy-start(bf16[2,72,256]{2,1,0:T(8,128)(2,1)} %param.15) | copy-start | bytes 221188
  21.0 589.1 %all-gather.43.cloned.1.call-start = ((), (), s32[]{:S(2)}) async-start(), calls=%async_computation.7 | async-start | bytes 16920576 | tf_op jit(solution)/shard_map/all_gather | solution.py:88
  21.8 72.7 %copy-start.20 = (s32[16]{0:T(128)S(1)}, s32[16]{0:T(128)}, u32[]{:S(2)}) copy-start(s32[16]{0:T(128)} %param.12) | copy-start | bytes 196
  21.8 72.8 %copy-start.13 = (bf16[2,72,256]{2,1,0:T(8,128)(2,1)S(1)}, bf16[2,72,256]{2,1,0:T(8,128)(2,1)}, u32[]{:S(2)}) copy-start(bf16[2,72,256]{2,1,0:T(8,128)(2,1)} %param.16) | copy-start | bytes 221188
  21.8 676.3 %all-gather.47.cloned.1.call-start = ((), (), s32[]{:S(2)}) async-start(), calls=%async_computation.9 | async-start | bytes 16920576 | tf_op jit(solution)/shard_map/all_gather | solution.py:88
  94.5 83.5 %copy-start.14 = (pred[16,64]{1,0:T(8,128)(4,1)}, pred[16,64]{1,0:T(8,128)(4,1)S(1)}, u32[]{:S(2)}) copy-start(pred[16,64]{1,0:T(8,128)(4,1)S(1)} %iota_compare_fusion.1) | copy-start | bytes 3076
  160.6 15.5 %copy-start.4 = (bf16[16,64,1,128]{3,1,0,2:T(8,128)(2,1)}, bf16[16,64,1,128]{3,1,0,2:T(8,128)(2,1)S(1)}, u32[]{:S(2)}) copy-start(bf16[16,64,1,128]{3,1,0,2:T(8,128)(2,1)S(1)} %get-tuple-element.29) | copy-start | bytes 786436
  160.6 15.5 %copy-start.6 = (bf16[16,64,1,128]{3,1,0,2:T(8,128)(2,1)}, bf16[16,64,1,128]{3,1,0,2:T(8,128)(2,1)S(1)}, u32[]{:S(2)}) copy-start(bf16[16,64,1,128]{3,1,0,2:T(8,128)(2,1)S(1)} %get-tuple-element.30) | copy-start | bytes 786436
  189.4 82.9 %copy-start.23 = (bf16[16,64,1152]{2,1,0:T(8,128)(2,1)}, bf16[16,64,1152]{2,1,0:T(8,128)(2,1)S(1)}, u32[]{:S(2)}) copy-start(bf16[16,64,1152]{2,1,0:T(8,128)(2,1)S(1)} %get-tuple-element.48) | copy-start | bytes 7077892
  304.7 93.0 %copy-start.17 = (f32[1152]{0:T(1024)S(1)}, f32[1152]{0:T(1024)}, u32[]{:S(2)}) copy-start(f32[1152]{0:T(1024)} %convert_add_fusion.5) | copy-start | bytes 13828
  404.9 5.7 copy-start.9
  421.1 5.2 copy-start.5
  421.1 5.2 copy-start.7
  423.9 10.2 %copy-start.2 = (bf16[16,64,1024]{2,1,0:T(8,128)(2,1)S(1)}, bf16[16,64,1024]{2,1,0:T(8,128)(2,1)}, u32[]{:S(2)}) copy-start(bf16[16,64,1024]{2,1,0:T(8,128)(2,1)} %reshape.307) | copy-start | bytes 6291460
  427.4 94.4 %copy-start.16 = (f32[1152]{0:T(1024)S(1)}, f32[1152]{0:T(1024)}, u32[]{:S(2)}) copy-start(f32[1152]{0:T(1024)} %convert_add_fusion.4) | copy-start | bytes 13828
  (10 other events, 25.7 us)
Sparse Core Ops, SparseCore 0:
  10.2 39.9 all-gather.28
  51.8 34.9 all-gather.30
  89.0 96.0 all-gather.34
  186.6 85.7 all-gather.32
  274.4 86.5 all-gather.36
  362.5 35.1 all-gather.38
  399.3 34.7 all-gather.40
  435.7 86.0 all-gather.44
  523.5 86.5 all-gather.42
  611.5 86.5 all-gather.46
where the time goes:
time: 739 us; the launch traced here: 731 us
  waiting for transfers between devices  333 us (45%)
  matrix products  206 us (28%)
  blocking collectives  131 us (18%)
  local copies, waits for them, and re-layouts  36.7 us (5%)
  between operations  15.5 us (2%)
  other arithmetic  8.82 us (1%)
    all_gather x10, waiting for transfers between devices, device_fn(): lax.all_gather(weight[layer_idx], 'w', axis=0, tiled=True)  329 us
    all_gather x4, blocking collectives, device_fn(): lax.all_gather(weight[layer_idx], 'w', axis=0, tiled=True)  77.8 us
    dot_general x2, matrix products, mlp_block(): jnp.einsum('bsd,df->bsf', normed, wg_full, preferred_element_type=jnp.flo...  63.7 us
    dot_general x2, matrix products, mlp_block(): jnp.einsum('bsf,fd->bsd', act_bf, wd_full, preferred_element_type=jnp.flo...  53.1 us
    unnamed x1, blocking collectives  53 us
    dot_general x2, matrix products, mlp_block(): jnp.einsum('bsd,df->bsf', normed, wu_full, preferred_element_type=jnp.flo...  52.9 us
  transfers between devices with their start and end apart: 10, of which 7 were waited for; matrix products, arithmetic and copies ran while one was open for 31% of the time, Pallas kernels for 0%

commit v1 on v0

v1 whole, which is shorter than its diff:
```python
import functools
import math

import jax
import jax.numpy as jnp
import numpy as np
from jax import lax
from jax.experimental import pallas as pl
from jax.experimental.pallas import tpu as pltpu
from jax.sharding import PartitionSpec as P

HEAD_DIM = 256
HALF = HEAD_DIM // 2
RMS_EPS = 1e-6
ROPE_THETA = 10000.0
MESH = pl.DeviceIdType.MESH
ROWS = 256
COL = 768
DCOL = 384
LAG = 2


def rms(x, gain):
    mean_sq = jnp.mean(x * x, axis=-1, keepdims=True)
    return (x * lax.rsqrt(mean_sq + RMS_EPS) * (1.0 + gain)).astype(jnp.bfloat16)


class Plan:
    def __init__(self, mesh, hidden, wq, wk, wv, wo, wg, wd):
        self.nw = mesh.shape["w"]
        self.nz = self.nw // 2
        self.side = math.isqrt(mesh.shape["dp"])
        self.layers = wq.shape[0]
        self.prompts, self.seq, self.width = hidden.shape
        self.tokens = self.prompts * self.seq
        self.kr = wq.shape[1]
        self.qw, self.kw = wq.shape[2], wk.shape[2]
        self.acols = self.qw + 2 * self.kw
        self.orow = wo.shape[1]
        self.ff = wg.shape[2]
        self.drow = wd.shape[1]
        self.na = self.ff // COL + 1
        self.nd = self.width // DCOL
        self.per_layer = self.na + 1 + self.nd
        self.steps = self.layers * self.per_layer
        self.heads = self.qw // HEAD_DIM


def body(pn, compute, len_ref, cos_ref, sin_ref, ag_ref, mg_ref, h_in, wq, wk, wv, wo, wg, wu, wd,
         out_h, out_k, out_v, la, lo, ld,
         h, r, q, kk, vv, o, a, wa, wob, wdb,
         own_sem, zs, zr, ps, pr, load_sem, io_sem):
    w = lax.axis_index("w")
    dp = lax.axis_index("dp")
    z, c = w // 2, w % 2
    nz = pn.nz
    gx, gy = dp // pn.side, dp % pn.side
    par = (gx + gy) % 2
    s = 1 - 2 * c
    up_w = lax.rem(z + 1, nz) * 2 + c
    dn_w = lax.rem(z + nz - 1, nz) * 2 + c
    far_w = lax.rem(z + s + nz, nz) * 2 + c
    mate_w = z * 2 + 1 - c
    x_dp = (gx + 1 - 2 * (gx % 2)) * pn.side + gy
    y_dp = gx * pn.side + gy + 1 - 2 * (gy % 2)
    dev_up, dev_dn, dev_far = (dp, up_w), (dp, dn_w), (dp, far_w)
    dev_mate, dev_x, dev_y = (dp, mate_w), (x_dp, w), (y_dp, w)
    farslot = nz // 2
    outs_up = [(0, 1), (1, 2), (2, 3)]
    outs_dn = [(0, 7), (7, 6), (6, 5)]

    barrier = pltpu.get_barrier_semaphore()
    for dev in (dev_up, dev_dn, dev_mate, dev_x, dev_y):
        pl.semaphore_signal(barrier, inc=1, device_id=dev, device_id_type=MESH)
    pl.semaphore_wait(barrier, 5)

    def split(g):
        return g // pn.per_layer, g % pn.per_layer

    def view_a(l, k, e, core, piece, half):
        off, size = {"all": (0, pn.acols), "half": (half * COL, COL), "x": (half * COL, COL // 2),
                     "y": (half * COL + COL // 2, COL // 2)}[piece]
        cols = slice(None) if piece == "all" else pl.ds(pl.multiple_of(off, 128), size)
        return la.at[l, k, e, pl.ds(pl.multiple_of(core * pn.kr, 8), pn.kr), cols]

    def view_o(l, k, e, core, piece, half):
        hr = pn.orow // 2
        off, size = {"all": (0, pn.orow), "half": (half * hr, hr), "x": (half * hr, hr // 2),
                     "y": (half * hr + hr // 2, hr // 2)}[piece]
        return lo.at[l, e, pl.ds(pl.multiple_of(core * pn.orow + off, 16), size), :]

    def view_d(l, k, e, core, piece, half):
        hr = pn.drow // 2
        hx = -(-hr // 16) * 8
        off, size = {"all": (0, pn.drow), "half": (half * hr, hr), "x": (half * hr, hx),
                     "y": (half * hr + hx, hr - hx)}[piece]
        return ld.at[l, k, e, pl.ds(pl.multiple_of(core * pn.drow + off, 8), size), :]

    def by_type(g, fn):
        l, i = split(g)

        @pl.when((i == 0) | ((i >= 2) & (i <= pn.na)))
        def _():
            fn(functools.partial(view_a, l, jnp.where(i == 0, 0, i - 1)))

        @pl.when(i == 1)
        def _():
            fn(functools.partial(view_o, l, 0))

        @pl.when(i > pn.na)
        def _():
            fn(functools.partial(view_d, l, i - pn.na - 1))

    def copy(src, dst, ss, rs, dev):
        return pltpu.make_async_remote_copy(src_ref=src, dst_ref=dst, send_sem=ss, recv_sem=rs,
                                            device_id=dev, device_id_type=MESH)

    def zsend(g, view, j, src, dst, dev):
        return copy(view(src, c, "half", par), view(dst, c, "half", par), zs.at[g, j], zr.at[g, j], dev)

    def arrived(g, view, j, slot):
        v = view(slot, c, "half", par)
        copy(v, v, zs.at[g, j], zr.at[g, j], dev_up).wait_recv()

    rest = pl.ds(1, nz - 1)

    def own_copies(l, i):
        me = pl.ds(pl.multiple_of(c * pn.kr, 8), pn.kr)
        if i == 0:
            return [(wq.at[l], la.at[l, 0, 0, me, pl.ds(0, pn.qw)]),
                    (wk.at[l], la.at[l, 0, 0, me, pl.ds(pn.qw, pn.kw)]),
                    (wv.at[l], la.at[l, 0, 0, me, pl.ds(pn.qw + pn.kw, pn.kw)])]
        if i == 1:
            return [(wo.at[l], view_o(l, 0, 0, c, "all", 0))]
        if i <= pn.na:
            k = i - 1
            return [(wg.at[l, :, pl.ds((k - 1) * COL, COL)], la.at[l, k, 0, me, pl.ds(0, COL)]),
                    (wu.at[l, :, pl.ds((k - 1) * COL, COL)], la.at[l, k, 0, me, pl.ds(COL, COL)])]
        k = i - pn.na - 1
        return [(wd.at[l, :, pl.ds(k * DCOL, DCOL)], view_d(l, k, 0, c, "all", 0))]

    for l in range(pn.layers):
        for i in range(pn.per_layer):
            for j, (src, dst) in enumerate(own_copies(l, i)):
                pltpu.make_async_copy(src, dst, own_sem.at[l * pn.per_layer + i]).start()

    def stage0(g):
        def fn(view):
            v = view(0, c, "all", 0)
            pltpu.make_async_copy(v, v, own_sem.at[g]).wait()
            zsend(g, view, 0, 0, 1, dev_up).start()
            zsend(g, view, 1, 0, nz - 1, dev_dn).start()
        by_type(g, fn)

    def stage_hop(n, g):
        def fn(view):
            arrived(g, view, 2 * n - 2, n)
            zsend(g, view, 2 * n, n, n + 1, dev_up).start()
            arrived(g, view, 2 * n - 1, nz - n)
            zsend(g, view, 2 * n + 1, nz - n, nz - n - 1, dev_dn).start()
            for j in (2 * n - 2, 2 * n - 1):
                zsend(g, view, j, 0, 1, dev_up).wait_send()
        by_type(g, fn)

    def stage3(g):
        def fn(view):
            arrived(g, view, 4, 3)
            arrived(g, view, 5, nz - 3)
            zsend(g, view, 6, farslot - s, farslot, dev_far).start()
            for j in (4, 5):
                zsend(g, view, j, 0, 1, dev_up).wait_send()
        by_type(g, fn)

    def xy(g, view, which, half, dev):
        v = view(rest, c, which, half)
        j = 0 if which == "x" else 1
        return copy(v, v, ps.at[g, j], pr.at[g, j], dev)

    def stage4(g):
        def fn(view):
            arrived(g, view, 6, farslot)
            xy(g, view, "x", par, dev_x).start()
            xy(g, view, "y", par, dev_y).start()
            zsend(g, view, 6, 0, 1, dev_up).wait_send()
        by_type(g, fn)

    def mate(g, view, core):
        v = view(slice(None), core, "all", 0)
        return copy(v, v, ps.at[g, 2], pr.at[g, 2], dev_mate)

    def stage5(g):
        def fn(view):
            xy(g, view, "x", 1 - par, dev_x).wait_recv()
            xy(g, view, "y", 1 - par, dev_y).wait_recv()
            mate(g, view, c).start()
            xy(g, view, "x", par, dev_x).wait_send()
            xy(g, view, "y", par, dev_y).wait_send()
        by_type(g, fn)

    def load_one(l, i, e):
        zz = lax.rem(z + nz - e, nz)

        def rows(n):
            return pl.ds(pl.multiple_of(zz * 2 * n, 16), 2 * n)
        return zz, rows

    def loads(g, go):
        l, i = split(g)

        @pl.when((i == 0) | ((i >= 2) & (i <= pn.na)))
        def _():
            k = jnp.where(i == 0, 0, i - 1)
            b = lax.rem(l * pn.na + k, 3)
            if go:
                for e in range(nz):
                    _, rows = load_one(l, i, e)
                    pltpu.make_async_copy(la.at[l, k, e], wa.at[b, rows(pn.kr), :], load_sem.at[b]).start()
            else:
                pltpu.make_async_copy(wa.at[b], wa.at[b], load_sem.at[b]).wait()

        @pl.when(i == 1)
        def _():
            if go:
                for e in range(nz):
                    _, rows = load_one(l, i, e)
                    pltpu.make_async_copy(lo.at[l, e], wob.at[rows(pn.orow), :], load_sem.at[3]).start()
            else:
                pltpu.make_async_copy(wob, wob, load_sem.at[3]).wait()

        @pl.when(i > pn.na)
        def _():
            k = i - pn.na - 1
            b = lax.rem(l * pn.nd + k, 2)
            if go:
                for e in range(nz):
                    _, rows = load_one(l, i, e)
                    pltpu.make_async_copy(ld.at[l, k, e], wdb.at[b, rows(pn.drow), :], load_sem.at[4 + b]).start()
            else:
                pltpu.make_async_copy(wdb.at[b], wdb.at[b], load_sem.at[4 + b]).wait()

    def stage6(g):
        def fn(view):
            mate(g, view, 1 - c).wait_recv()
            mate(g, view, c).wait_send()
        by_type(g, fn)
        loads(g, True)

    tiles = pn.tokens // ROWS

    def tile(t):
        return pl.ds(pl.multiple_of(t * ROWS, ROWS), ROWS)

    def unit_qkv(l):
        b = lax.rem(l * pn.na, 3)
        gain = ag_ref[l]

        def step(t, _):
            rr = tile(t)
            normed = rms(h[rr, :].astype(jnp.float32), gain)
            cos, sin = cos_ref[...], sin_ref[...]

            def rope(p):
                first, second = p[:, :HALF], p[:, HALF:]
                return first * cos - second * sin, second * cos + first * sin
            for hh in range(pn.heads):
                cols = pl.ds(hh * HEAD_DIM, HEAD_DIM)
                first, second = rope(jnp.dot(normed, wa[b, :, cols], preferred_element_type=jnp.float32))
                q[rr, pl.ds(hh * HEAD_DIM, HALF)] = (first * HEAD_DIM ** -0.5).astype(jnp.bfloat16)
                q[rr, pl.ds(hh * HEAD_DIM + HALF, HALF)] = (second * HEAD_DIM ** -0.5).astype(jnp.bfloat16)
            first, second = rope(jnp.dot(normed, wa[b, :, pl.ds(pn.qw, pn.kw)], preferred_element_type=jnp.float32))
            kk[l, rr, pl.ds(0, HALF)] = first.astype(jnp.bfloat16)
            kk[l, rr, pl.ds(HALF, HALF)] = second.astype(jnp.bfloat16)
            vv[l, rr, :] = jnp.dot(normed, wa[b, :, pl.ds(pn.qw + pn.kw, pn.kw)],
                                   preferred_element_type=jnp.float32).astype(jnp.bfloat16)
            return 0
        lax.fori_loop(0, tiles, step, 0)
        for j, (src, dst) in enumerate(((kk, out_k), (vv, out_v))):
            pltpu.make_async_copy(src.at[l], dst.at[l], io_sem.at[1 + 2 * l + j]).start()

    def unit_attn(l, lo_pair, hi_pair):
        two = 2 * pn.seq
        shape = (pn.heads * two, two)
        row = lax.broadcasted_iota(jnp.int32, shape, 0) % two
        col = lax.broadcasted_iota(jnp.int32, shape, 1)
        rp, cp = row // pn.seq, col // pn.seq
        qpos, kpos = row % pn.seq, col % pn.seq
        causal = (rp == cp) & (kpos <= qpos)

        def step(t, _):
            rr = pl.ds(pl.multiple_of(t * two, two), two)
            len0, len1 = len_ref[2 * t], len_ref[2 * t + 1]
            qs = q[rr, :]
            stacked = jnp.concatenate([qs[:, i * HEAD_DIM:(i + 1) * HEAD_DIM] for i in range(pn.heads)], axis=0)
            sc = lax.dot_general(stacked, kk[l, rr, :], (((1,), (1,)), ((), ())), preferred_element_type=jnp.float32)
            allowed = causal & (kpos < jnp.where(cp == 0, len0, len1))
            sc = jnp.where(allowed, sc, -1e30)
            sc = jnp.exp(sc - jnp.max(sc, axis=-1, keepdims=True))
            pr_ = sc / jnp.sum(sc, axis=-1, keepdims=True)
            live = qpos < jnp.where(rp == 0, len0, len1)
            pr_ = jnp.where(live, pr_, 0.0).astype(jnp.bfloat16)
            ov = jnp.dot(pr_, vv[l, rr, :], preferred_element_type=jnp.float32).astype(jnp.bfloat16)
            for i in range(pn.heads):
                o[rr, pl.ds(i * HEAD_DIM, HEAD_DIM)] = ov[i * two:(i + 1) * two, :]
            return 0
        lax.fori_loop(lo_pair, hi_pair, step, 0)

    def unit_o(l):
        gain = mg_ref[l]

        def step(t, _):
            rr = tile(t)
            mixed = h[rr, :].astype(jnp.float32) + jnp.dot(o[rr, :], wob[...], preferred_element_type=jnp.float32)
            mixed = mixed.astype(jnp.bfloat16)
            h[rr, :] = mixed
            r[rr, :] = rms(mixed.astype(jnp.float32), gain)
            return 0
        lax.fori_loop(0, tiles, step, 0)

    def unit_mlp(l, k):
        b = lax.rem(l * pn.na + k, 3)

        def step(t, _):
            rr = tile(t)
            x = r[rr, :]
            for j in range(COL // 256):
                gp = jnp.dot(x, wa[b, :, pl.ds(j * 256, 256)], preferred_element_type=jnp.float32)
                upv = jnp.dot(x, wa[b, :, pl.ds(COL + j * 256, 256)], preferred_element_type=jnp.float32)
                act = (jax.nn.gelu(gp, approximate=True) * upv).astype(jnp.bfloat16)
                a[rr, pl.ds(pl.multiple_of((k - 1) * COL + j * 256, 256), 256)] = act
            return 0
        lax.fori_loop(0, tiles, step, 0)

    def unit_down(l, k):
        b = lax.rem(l * pn.nd + k, 2)
        cols = pl.ds(pl.multiple_of(k * DCOL, 128), DCOL)

        def step(t, _):
            rr = tile(t)
            acc = jnp.dot(a[rr, :], wdb[b], preferred_element_type=jnp.float32)
            h[rr, cols] = (h[rr, cols].astype(jnp.float32) + acc).astype(jnp.bfloat16)
            return 0
        lax.fori_loop(0, tiles, step, 0)

    pairs = pn.prompts // 2
    pltpu.make_async_copy(h_in, h, io_sem.at[0]).start()
    pltpu.make_async_copy(h_in, h, io_sem.at[0]).wait()

    last = 6 * LAG

    def run_units(t):
        g = t - last - 1
        l, i = split(g)
        g2 = g - 1
        l2, i2 = split(g2)

        @pl.when((g >= 0) & (g < pn.steps))
        def _():
            loads(g, False)

        if not compute:
            return

        @pl.when((g2 >= 0) & (i2 >= 2) & (i2 <= pn.na))
        def _():
            unit_mlp(l2, i2 - 1)

        @pl.when((g >= 0) & (g < pn.steps))
        def _():
            @pl.when(i == 0)
            def _():
                unit_qkv(l)

            @pl.when(i == 1)
            def _():
                unit_attn(l, 0, pairs // 2)

            @pl.when(i == 2)
            def _():
                unit_attn(l, pairs // 2, pairs)
                unit_o(l)

            @pl.when(i > pn.na)
            def _():
                unit_down(l, i - pn.na - 1)

    stages = [stage0, functools.partial(stage_hop, 1), functools.partial(stage_hop, 2), stage3, stage4, stage5, stage6]

    def tick(t, _):
        for n in range(len(stages) - 1, -1, -1):
            g = t - n * LAG

            @pl.when((g >= 0) & (g < pn.steps))
            def _(n=n, g=g):
                stages[n](g)
        run_units(t)
        return 0
    lax.fori_loop(0, pn.steps + last + 1, tick, 0)

    out = pltpu.make_async_copy(h, out_h, io_sem.at[0])
    out.start()
    if compute:
        for l in range(pn.layers):
            for j, (src, dst) in enumerate(((kk, out_k), (vv, out_v))):
                pltpu.make_async_copy(src.at[l], dst.at[l], io_sem.at[1 + 2 * l + j]).wait()
    out.wait()


def make(mesh, compute=True):
    batch_spec = P(('dp', 'w'))
    weight_spec = P(None, 'w')
    cache_spec = P(None, ('dp', 'w'))

    def device_fn(hidden, lengths, attn_norm, w_q, w_k, w_v, w_o, mlp_norm, w_gate, w_up, w_down):
        pn = Plan(mesh, hidden, w_q, w_k, w_v, w_o, w_gate, w_down)
        norms = lax.all_gather(jnp.stack([attn_norm, mlp_norm]), 'w', axis=2, tiled=True)
        norms = norms.astype(jnp.float32)[:, :, None, :]
        inv_freq = np.float32(ROPE_THETA) ** (np.float32(-2.0) * np.arange(HALF, dtype=np.float32) / np.float32(HEAD_DIM))
        angles = np.arange(pn.seq, dtype=np.float32)[:, None] * inv_freq[None, :].astype(np.float32)
        reps = ROWS // pn.seq
        cos = jnp.asarray(np.tile(np.cos(angles).astype(np.float32), (reps, 1)))
        sin = jnp.asarray(np.tile(np.sin(angles).astype(np.float32), (reps, 1)))
        bf = jnp.bfloat16
        nz, S = pn.nz, jax.ShapeDtypeStruct
        L, T = pn.layers, pn.tokens
        vm = pl.BlockSpec(memory_space=pltpu.VMEM)
        anyspec = pl.BlockSpec(memory_space=pl.ANY)
        outs = pl.pallas_call(
            functools.partial(body, pn, compute),
            name="layers",
            out_shape=(S((T, pn.width), bf), S((L, T, pn.kw), bf), S((L, T, pn.kw), bf),
                       S((L, pn.na, nz, 2 * pn.kr, pn.acols), bf),
                       S((L, nz, 2 * pn.orow, pn.width), bf),
                       S((L, pn.nd, nz, 2 * pn.drow, DCOL), bf)),
            in_specs=[pl.BlockSpec(memory_space=pltpu.SMEM), vm, vm, vm, vm] + [anyspec] * 8,
            out_specs=(anyspec,) * 6,
            scratch_shapes=[
                pltpu.VMEM((T, pn.width), bf), pltpu.VMEM((T, pn.width), bf),
                pltpu.VMEM((T, pn.qw), bf), pltpu.VMEM((L, T, pn.kw), bf), pltpu.VMEM((L, T, pn.kw), bf),
                pltpu.VMEM((T, pn.qw), bf), pltpu.VMEM((T, pn.ff), bf),
                pltpu.VMEM((3, pn.width, pn.acols), bf), pltpu.VMEM((pn.qw, pn.width), bf),
                pltpu.VMEM((2, pn.ff, DCOL), bf),
                pltpu.SemaphoreType.DMA((pn.steps,)),
                pltpu.SemaphoreType.DMA((pn.steps, nz - 1)), pltpu.SemaphoreType.DMA((pn.steps, nz - 1)),
                pltpu.SemaphoreType.DMA((pn.steps, 3)), pltpu.SemaphoreType.DMA((pn.steps, 3)),
                pltpu.SemaphoreType.DMA((6,)), pltpu.SemaphoreType.DMA((1 + 2 * L,)),
            ],
            compiler_params=pltpu.CompilerParams(collective_id=0, has_side_effects=True, vmem_limit_bytes=63 << 20),
        )(lengths, cos, sin, norms[0], norms[1], hidden.reshape(T, pn.width), w_q, w_k, w_v, w_o, w_gate, w_up, w_down)
        cache = (L, pn.prompts, pn.seq, pn.kw // HEAD_DIM, HEAD_DIM)
        return outs[0].reshape(hidden.shape), outs[1].reshape(cache), outs[2].reshape(cache)

    return jax.shard_map(device_fn, mesh=mesh, in_specs=(batch_spec, batch_spec) + (weight_spec,) * 9,
                         out_specs=(batch_spec, cache_spec, cache_spec), check_vma=False)


def solution(mesh):
    return make(mesh)
```

time: 739 us -> 396 us (0.54)
  Pallas kernels: 0 us -> 365 us
  waiting for transfers between devices: 333 us -> 0 us
  matrix products: 206 us -> 0 us
  blocking collectives: 131 us -> 23.1 us
  local copies, waits for them, and re-layouts: 36.7 us -> 6.64 us
  between operations: 15.5 us -> 0.67 us
  other arithmetic: 8.82 us -> 0.7 us
    pallas_call x0 -> x1, Pallas kernels: none -> 365 us  [device_fn(): pl.pallas_call(functools.partial(body, pn, compute), name='layers', out_s...]
    all_gather x10 -> x0, waiting for transfers between devices: 329 us -> none  [device_fn(): lax.all_gather(weight[layer_idx], 'w', axis=0, tiled=True)]
    dot_general x18 -> x0, matrix products: 206 us -> none  [the longest x2 63.7 us: mlp_block(): jnp.einsum('bsd,df->bsf', normed, wg_full, preferred_element_type=jnp.flo...]
    all_gather x4 -> x1, blocking collectives: 77.8 us -> 23.1 us  [device_fn(): lax.all_gather(jnp.stack([attn_norm, mlp_norm]), 'w', axis=2, tiled=True)]
    unnamed x1 -> x0, blocking collectives: 53 us -> none
    reshape x4 -> x0, local copies, waits for them, and re-layouts: 16.9 us -> none  [the longest x2 11.4 us: layer_body(): jnp.einsum('bsd,de->bse', normed, wq_full, preferred_element_type=jnp.flo...]
    slice x9 -> x0, local copies, waits for them, and re-layouts: 14.6 us -> none  [the longest x7 10.8 us: device_fn(): weight[layer_idx]]
  transfers between devices with their start and end apart: 10 -> 0, of which waited for: 7 -> 0; matrix products, arithmetic and copies ran while one was open for 31% -> 0% of each run, Pallas kernels for 0% -> 0%
where the time goes in v1:
time: 396 us
  Pallas kernels  365 us (92%)
  blocking collectives  23.1 us (6%)
  local copies, waits for them, and re-layouts  6.64 us (2%)
    pallas_call x1, Pallas kernels, device_fn(): pl.pallas_call(functools.partial(body, pn, compute), name='layers', out_s...  365 us
    all_gather x1, blocking collectives, device_fn(): lax.all_gather(jnp.stack([attn_norm, mlp_norm]), 'w', axis=2, tiled=True)  23.1 us

profile of v1, /device:TPU:30, one launch (start us, length us, event | category | flops | bytes accessed | tf_op | source)
XLA Modules:
  0.0 395.7 jit_solution(17083514889446171517)
XLA Ops:
  0.6 0.7 pad_maximum_fusion
  1.3 0.1 copy.23
  1.4 23.1 %all_gather.3 = bf16[2,2,1152]{1,0,2:T(2,128)(2,1)S(1)} all-gather(bf16[2,2,72]{1,0,2:T(2,128)(2,1)S(1)} %copy.23), channel_id=1, replica_groups=mesh['dp'=4,'w'=16] {'w'}, dimensions={2}, use_global_device_ids=true | all-gather | bytes 9792 | tf_op jit(solution)/shard_map/all_gather | solution.py:415
  24.5 0.5 copy.24
  25.1 0.6 slice_bitcast_fusion
  25.7 364.6 %layers.1 = (bf16[1024,1152]{1,0:T(8,128)(2,1)}, bf16[2,1024,256]{2,1,0:T(8,128)(2,1)}, bf16[2,1024,256]{2,1,0:T(8,128)(2,1)}, bf16[2,10,8,144,1536]{4,3,2,1,0:T...) custom-call(s32[16]{0:T(128)} %len_ref.1, f32[256,128]{1,0:T(8,128)} %constant.4.clone.cos_ref, ...), custom_call_target="tpu_custom_call" | custom-call | tf_op jit(solution)/shard_map/layers/pallas_call | solution.py:427
  390.3 0.0 copy-start.1
  390.3 0.0 copy-start
  390.3 3.4 copy.30
  393.8 0.0 copy-done.1
  393.8 1.0 copy.31
  394.7 0.0 copy-done
  394.7 1.0 copy.32
  (1 shorter events, 0.0 us)
Async XLA Ops:
  390.3 3.4 copy-start.1
  390.3 4.4 %copy-start = (bf16[2,1024,256]{2,1,0:T(8,128)(2,1)S(1)}, bf16[2,1024,256]{2,1,0:T(8,128)(2,1)}, u32[]{:S(2)}) copy-start(bf16[2,1024,256]{2,1,0:T(8,128)(2,1)} %get-tuple-element.8) | copy-start | bytes 3145732
